TPU v7x, 32 devices: a whole 2x2x4 slice. The times are simulated.
32 devices in a mesh: gx: 8 (over y, x, core), gy: 4 (over z).
Axes of the slice: x: 2, y: 2, z: 4, core: 2. Of those that a mesh axis runs over, the one named last changes fastest.
Arguments:
- signals: float32 [16, 32, 16, 128], P('gx', 'gy'), may hold values from -6 to 6
- tiles: bfloat16 [16, 32, 4, 128, 128], P('gx', 'gy'), may hold values from 0 to 0.00390625
- tile_dir: int32 [16, 32, 4], P('gx', 'gy'), may hold values from 0 to 8
- tile_mask: int32 [16, 32, 4], P('gx', 'gy'), may hold values 0 or 1
- live_rows: int32 [16, 32], P('gx', 'gy'), may hold values from 32 to 128
- bound_rows: int32 [16, 32], P('gx', 'gy'), may hold values from 1 to 32, as said below
- scale_coeffs: float32 [6, 5], replicated, may hold values from -1 to 1
- spectral_bound: float32 [1], replicated, may hold values from 2.5 to 4
Outputs:
- coefficients: float32 [6, 16, 32, 16, 128], P(None, 'gx', 'gy')
- energy: float32 [6, 16], replicated
Inputs may be any that keep to these rules, and one draw needn't show every extreme that they name: `bound_rows`: in every draw, some blocks on every device have exactly 32 boundary rows.
All inputs are finite; a program needn't handle non-finite values. No bound on the sum of `tile_mask` on one device may be relied on, other than what follows from the above.
Results may differ from a plain program's by a relative error of at most 0.0003.
Values may be sent and summed in bfloat16 or wider, within the bound.
A program may use at most 64 MiB of HBM per device.

v0:
```python
import jax
import jax.numpy as jnp
from jax import lax
from jax.sharding import PartitionSpec as P

DEG = 4


def with_halo(array, sides, width):
    for axis, dim in sides:
        devices, length = (lax.axis_size(axis), array.shape[dim])
        up = [(i, (i + 1) % devices) for i in range(devices - 1)]
        down = [(j, i) for i, j in up]
        last = lax.slice_in_dim(array, length - width, length, axis=dim)
        first = lax.slice_in_dim(array, 0, width, axis=dim)
        before = lax.ppermute(last, axis, up)
        after = lax.ppermute(first, axis, down)
        array = jnp.concatenate([before, array, after], axis=dim)
    return array


def scaled_laplacian(values, adjacent, degree, factor):
    return factor * (degree * values - adjacent) - values


def shards(
    signals, tiles, tile_dir, tile_mask, live_rows, bound_rows, scale_coeffs, spectral_bound
):
    tile_size = signals.shape[3]
    extent_x = signals.shape[0]
    extent_y = signals.shape[1]
    slot_count = tiles.shape[2]
    block_count = extent_x * extent_y
    positions = lax.broadcasted_iota(jnp.int32, (1, 1, tile_size), 2)
    live_ind = (positions < live_rows[:, :, None]).astype(jnp.float32)
    bound_ind = (positions < bound_rows[:, :, None]).astype(jnp.float32)
    flat_tiles = tiles.reshape(block_count, slot_count, tile_size, tile_size)

    def adjacency(values):
        own_rows = values.astype(jnp.bfloat16)
        edge_rows = (values * bound_ind[:, :, None, :]).astype(jnp.bfloat16)
        padded = with_halo(edge_rows, (("gx", 0), ("gy", 1)), 1)
        slot_list = []
        for slot_index in range(slot_count):
            picked = jnp.zeros_like(own_rows)
            for direction in range(9):
                step_x = direction // 3 - 1
                step_y = direction % 3 - 1
                if direction == 4:
                    source = own_rows
                else:
                    source = padded[
                        1 + step_x : 1 + step_x + extent_x, 1 + step_y : 1 + step_y + extent_y
                    ]
                matches = (tile_dir[:, :, slot_index] == direction)[:, :, None, None]
                picked = jnp.where(matches, source, picked)
            kept = (tile_mask[:, :, slot_index] == 1)[:, :, None, None]
            picked = jnp.where(kept, picked, jnp.zeros_like(picked))
            slot_list.append(picked)
        inputs = jnp.stack(slot_list, axis=1 + 1)
        flat_inputs = inputs.reshape(block_count, slot_count, inputs.shape[3], tile_size)
        product = lax.dot_general(
            flat_inputs,
            flat_tiles,
            (((1, 3), (1, 3)), ((0,), (0,))),
            preferred_element_type=jnp.float32,
        )
        product = product.reshape(extent_x, extent_y, inputs.shape[3], tile_size)
        return product * live_ind[:, :, None, :]

    channels = signals.shape[2]
    initial = signals * live_ind[:, :, None, :]
    joined = jnp.concatenate([initial, live_ind[:, :, None, :]], axis=2)
    first_pass = adjacency(joined)
    degree = first_pass[:, :, channels:, :]
    factor = 2.0 / spectral_bound[0]
    previous = initial
    current = scaled_laplacian(initial, first_pass[:, :, :channels, :], degree, factor)
    totals = 0.5 * scale_coeffs[:, 0][:, None, None, None, None] * initial[None]
    totals = totals + scale_coeffs[:, 1][:, None, None, None, None] * current[None]
    for degree_index in range(2, DEG + 1):
        adjacent = adjacency(current)
        following = 2.0 * scaled_laplacian(current, adjacent, degree, factor) - previous
        previous = current
        current = following
        totals = totals + scale_coeffs[:, degree_index][:, None, None, None, None] * current[None]
    nodes = extent_x * extent_y * tile_size * lax.axis_size("gx") * lax.axis_size("gy")
    local_sums = jnp.sum(totals * totals, axis=(1, 2, 4))
    energy = lax.psum(local_sums, ("gx", "gy")) / nodes
    return (totals, energy)


def solution(mesh):
    placed = (
        P("gx", "gy", None, None),
        P("gx", "gy", None, None, None),
        P("gx", "gy", None),
        P("gx", "gy", None),
        P("gx", "gy"),
        P("gx", "gy"),
        P(),
        P(),
    )
    return jax.shard_map(
        shards,
        mesh=mesh,
        in_specs=placed,
        out_specs=(P(None, "gx", "gy", None, None), P()),
        check_vma=False,
    )
```

profile of v0, /device:TPU:0, one launch (start us, length us, event | category | flops | bytes accessed | tf_op | source)
XLA Modules:
  0.0 117.8 jit_solution(2510925606802948596)
XLA Ops:
  3.3 2.4 %collective-permute-start = (bf16[1,8,17,128]{3,2,1,0:T(8,128)(2,1)S(1)}, bf16[1,8,17,128]{3,2,1,0:T(8,128)(2,1)S(1)}, u32[]{:S(2)}, u32[]{:S(2)}) collective-permute-start(bf16[1,8,17,128]{3,2,1,0:T(8,128)(2,1)S(1)} %get-tuple-element.37), channel_id=1, source_target_pairs={{0,4},{4,8},{8,12},{12,16},{16,20},{20,24},{24,28},{1,5},{5,9},{9,... | collective-permute-start | bytes 104456 | tf_op jit(solution)/shard_map/ppermute | solution.py:16
  5.7 1.3 %collective-permute-start.1 = (bf16[1,8,17,128]{3,2,1,0:T(8,128)(2,1)S(1)}, bf16[1,8,17,128]{3,2,1,0:T(8,128)(2,1)S(1)}, u32[]{:S(2)}, u32[]{:S(2)}) collective-permute-start(bf16[1,8,17,128]{3,2,1,0:T(8,128)(2,1)S(1)} %get-tuple-element.38), channel_id=1, source_target_pairs={{4,0},{8,4},{12,8},{16,12},{20,16},{24,20},{28,24},{5,1},{9,5},{13... | collective-permute-start | bytes 104456 | tf_op jit(solution)/shard_map/ppermute | solution.py:17
  10.9 1.3 %collective-permute-start.2 = (bf16[4,1,17,128]{3,2,1,0:T(8,128)(2,1)S(1)}, bf16[4,1,17,128]{3,2,1,0:T(8,128)(2,1)S(1)}, u32[]{:S(2)}, u32[]{:S(2)}) collective-permute-start(bf16[4,1,17,128]{3,2,1,0:T(8,128)(2,1)S(1)} %get-tuple-element.23), channel_id=1, source_target_pairs={{1,0},{2,1},{3,2},{5,4},{6,5},{7,6},{9,8},{10,9},{11,10},{13,12},{... | collective-permute-start | bytes 52232 | tf_op jit(solution)/shard_map/ppermute | solution.py:17
  12.2 4.5 %collective-permute-start.3 = (bf16[4,1,17,128]{3,2,1,0:T(8,128)(2,1)S(1)}, bf16[4,1,17,128]{3,2,1,0:T(8,128)(2,1)S(1)}, u32[]{:S(2)}, u32[]{:S(2)}) collective-permute-start(bf16[4,1,17,128]{3,2,1,0:T(8,128)(2,1)S(1)} %get-tuple-element.24), channel_id=1, source_target_pairs={{0,1},{1,2},{2,3},{4,5},{5,6},{6,7},{8,9},{9,10},{10,11},{12,13},{... | collective-permute-start | bytes 52232 | tf_op jit(solution)/shard_map/ppermute | solution.py:16
  20.2 3.6 %collective-permute-start.4 = (bf16[1,8,16,128]{3,2,1,0:T(8,128)(2,1)S(1)}, bf16[1,8,16,128]{3,2,1,0:T(8,128)(2,1)S(1)}, u32[]{:S(2)}, u32[]{:S(2)}) collective-permute-start(bf16[1,8,16,128]{3,2,1,0:T(8,128)(2,1)S(1)} %get-tuple-element.43), channel_id=1, source_target_pairs={{0,4},{4,8},{8,12},{12,16},{16,20},{20,24},{24,28},{1,5},{5,9},{9,... | collective-permute-start | bytes 98312 | tf_op jit(solution)/shard_map/ppermute | solution.py:16
  23.8 1.3 %collective-permute-start.5 = (bf16[1,8,16,128]{3,2,1,0:T(8,128)(2,1)S(1)}, bf16[1,8,16,128]{3,2,1,0:T(8,128)(2,1)S(1)}, u32[]{:S(2)}, u32[]{:S(2)}) collective-permute-start(bf16[1,8,16,128]{3,2,1,0:T(8,128)(2,1)S(1)} %get-tuple-element.44), channel_id=1, source_target_pairs={{4,0},{8,4},{12,8},{16,12},{20,16},{24,20},{28,24},{5,1},{9,5},{13... | collective-permute-start | bytes 98312 | tf_op jit(solution)/shard_map/ppermute | solution.py:17
  25.1 3.5 %collective-permute-done.5 = bf16[1,8,16,128]{3,2,1,0:T(8,128)(2,1)S(1)} collective-permute-done((bf16[1,8,16,128]{3,2,1,0:T(8,128)(2,1)S(1)}, bf16[1,8,16,128]{3,2,1,0:T(8,128)(2,1)S(1)}, u32[]{:S(2)}, u32[]{:S(2)}) %collective-permute-start.5) | collective-permute-done | bytes 32800 | tf_op jit(solution)/shard_map/ppermute | solution.py:17
  28.6 1.3 %collective-permute-start.6 = (bf16[4,1,16,128]{3,2,1,0:T(8,128)(2,1)S(1)}, bf16[4,1,16,128]{3,2,1,0:T(8,128)(2,1)S(1)}, u32[]{:S(2)}, u32[]{:S(2)}) collective-permute-start(bf16[4,1,16,128]{3,2,1,0:T(8,128)(2,1)S(1)} %get-tuple-element.35), channel_id=1, source_target_pairs={{1,0},{2,1},{3,2},{5,4},{6,5},{7,6},{9,8},{10,9},{11,10},{13,12},{... | collective-permute-start | bytes 49160 | tf_op jit(solution)/shard_map/ppermute | solution.py:17
  29.9 4.9 %collective-permute-start.7 = (bf16[4,1,16,128]{3,2,1,0:T(8,128)(2,1)S(1)}, bf16[4,1,16,128]{3,2,1,0:T(8,128)(2,1)S(1)}, u32[]{:S(2)}, u32[]{:S(2)}) collective-permute-start(bf16[4,1,16,128]{3,2,1,0:T(8,128)(2,1)S(1)} %get-tuple-element.36), channel_id=1, source_target_pairs={{0,1},{1,2},{2,3},{4,5},{5,6},{6,7},{8,9},{9,10},{10,11},{12,13},{... | collective-permute-start | bytes 49160 | tf_op jit(solution)/shard_map/ppermute | solution.py:16
  34.8 1.4 %collective-permute-done.7 = bf16[4,1,16,128]{3,2,1,0:T(8,128)(2,1)S(1)} collective-permute-done((bf16[4,1,16,128]{3,2,1,0:T(8,128)(2,1)S(1)}, bf16[4,1,16,128]{3,2,1,0:T(8,128)(2,1)S(1)}, u32[]{:S(2)}, u32[]{:S(2)}) %collective-permute-start.7) | collective-permute-done | bytes 16416 | tf_op jit(solution)/shard_map/ppermute | solution.py:16
  38.0 3.7 %collective-permute-start.8 = (bf16[1,8,16,128]{3,2,1,0:T(8,128)(2,1)S(1)}, bf16[1,8,16,128]{3,2,1,0:T(8,128)(2,1)S(1)}, u32[]{:S(2)}, u32[]{:S(2)}) collective-permute-start(bf16[1,8,16,128]{3,2,1,0:T(8,128)(2,1)S(1)} %get-tuple-element.41), channel_id=1, source_target_pairs={{0,4},{4,8},{8,12},{12,16},{16,20},{20,24},{24,28},{1,5},{5,9},{9,... | collective-permute-start | bytes 98312 | tf_op jit(solution)/shard_map/ppermute | solution.py:16
  41.7 1.3 %collective-permute-start.9 = (bf16[1,8,16,128]{3,2,1,0:T(8,128)(2,1)S(1)}, bf16[1,8,16,128]{3,2,1,0:T(8,128)(2,1)S(1)}, u32[]{:S(2)}, u32[]{:S(2)}) collective-permute-start(bf16[1,8,16,128]{3,2,1,0:T(8,128)(2,1)S(1)} %get-tuple-element.42), channel_id=1, source_target_pairs={{4,0},{8,4},{12,8},{16,12},{20,16},{24,20},{28,24},{5,1},{9,5},{13... | collective-permute-start | bytes 98312 | tf_op jit(solution)/shard_map/ppermute | solution.py:17
  43.0 2.2 %collective-permute-done.9 = bf16[1,8,16,128]{3,2,1,0:T(8,128)(2,1)S(1)} collective-permute-done((bf16[1,8,16,128]{3,2,1,0:T(8,128)(2,1)S(1)}, bf16[1,8,16,128]{3,2,1,0:T(8,128)(2,1)S(1)}, u32[]{:S(2)}, u32[]{:S(2)}) %collective-permute-start.9) | collective-permute-done | bytes 32800 | tf_op jit(solution)/shard_map/ppermute | solution.py:17
  45.2 1.3 %collective-permute-start.10 = (bf16[4,1,16,128]{3,2,1,0:T(8,128)(2,1)S(1)}, bf16[4,1,16,128]{3,2,1,0:T(8,128)(2,1)S(1)}, u32[]{:S(2)}, u32[]{:S(2)}) collective-permute-start(bf16[4,1,16,128]{3,2,1,0:T(8,128)(2,1)S(1)} %get-tuple-element.31), channel_id=1, source_target_pairs={{1,0},{2,1},{3,2},{5,4},{6,5},{7,6},{9,8},{10,9},{11,10},{13,12},{... | collective-permute-start | bytes 49160 | tf_op jit(solution)/shard_map/ppermute | solution.py:17
  46.4 4.8 %collective-permute-start.11 = (bf16[4,1,16,128]{3,2,1,0:T(8,128)(2,1)S(1)}, bf16[4,1,16,128]{3,2,1,0:T(8,128)(2,1)S(1)}, u32[]{:S(2)}, u32[]{:S(2)}) collective-permute-start(bf16[4,1,16,128]{3,2,1,0:T(8,128)(2,1)S(1)} %get-tuple-element.32), channel_id=1, source_target_pairs={{0,1},{1,2},{2,3},{4,5},{5,6},{6,7},{8,9},{9,10},{10,11},{12,13},{... | collective-permute-start | bytes 49160 | tf_op jit(solution)/shard_map/ppermute | solution.py:16
  51.3 1.4 %collective-permute-done.11 = bf16[4,1,16,128]{3,2,1,0:T(8,128)(2,1)S(1)} collective-permute-done((bf16[4,1,16,128]{3,2,1,0:T(8,128)(2,1)S(1)}, bf16[4,1,16,128]{3,2,1,0:T(8,128)(2,1)S(1)}, u32[]{:S(2)}, u32[]{:S(2)}) %collective-permute-start.11) | collective-permute-done | bytes 16416 | tf_op jit(solution)/shard_map/ppermute | solution.py:16
  54.5 4.1 %collective-permute-start.12 = (bf16[1,8,16,128]{3,2,1,0:T(8,128)(2,1)S(1)}, bf16[1,8,16,128]{3,2,1,0:T(8,128)(2,1)S(1)}, u32[]{:S(2)}, u32[]{:S(2)}) collective-permute-start(bf16[1,8,16,128]{3,2,1,0:T(8,128)(2,1)S(1)} %get-tuple-element.39), channel_id=1, source_target_pairs={{0,4},{4,8},{8,12},{12,16},{16,20},{20,24},{24,28},{1,5},{5,9},{9,... | collective-permute-start | bytes 98312 | tf_op jit(solution)/shard_map/ppermute | solution.py:16
  58.6 1.3 %collective-permute-start.13 = (bf16[1,8,16,128]{3,2,1,0:T(8,128)(2,1)S(1)}, bf16[1,8,16,128]{3,2,1,0:T(8,128)(2,1)S(1)}, u32[]{:S(2)}, u32[]{:S(2)}) collective-permute-start(bf16[1,8,16,128]{3,2,1,0:T(8,128)(2,1)S(1)} %get-tuple-element.40), channel_id=1, source_target_pairs={{4,0},{8,4},{12,8},{16,12},{20,16},{24,20},{28,24},{5,1},{9,5},{13... | collective-permute-start | bytes 98312 | tf_op jit(solution)/shard_map/ppermute | solution.py:17
  59.9 2.4 %collective-permute-done.13 = bf16[1,8,16,128]{3,2,1,0:T(8,128)(2,1)S(1)} collective-permute-done((bf16[1,8,16,128]{3,2,1,0:T(8,128)(2,1)S(1)}, bf16[1,8,16,128]{3,2,1,0:T(8,128)(2,1)S(1)}, u32[]{:S(2)}, u32[]{:S(2)}) %collective-permute-start.13) | collective-permute-done | bytes 32800 | tf_op jit(solution)/shard_map/ppermute | solution.py:17
  62.4 1.3 %collective-permute-start.14 = (bf16[4,1,16,128]{3,2,1,0:T(8,128)(2,1)S(1)}, bf16[4,1,16,128]{3,2,1,0:T(8,128)(2,1)S(1)}, u32[]{:S(2)}, u32[]{:S(2)}) collective-permute-start(bf16[4,1,16,128]{3,2,1,0:T(8,128)(2,1)S(1)} %get-tuple-element.27), channel_id=1, source_target_pairs={{1,0},{2,1},{3,2},{5,4},{6,5},{7,6},{9,8},{10,9},{11,10},{13,12},{... | collective-permute-start | bytes 49160 | tf_op jit(solution)/shard_map/ppermute | solution.py:17
  63.6 4.8 %collective-permute-start.15 = (bf16[4,1,16,128]{3,2,1,0:T(8,128)(2,1)S(1)}, bf16[4,1,16,128]{3,2,1,0:T(8,128)(2,1)S(1)}, u32[]{:S(2)}, u32[]{:S(2)}) collective-permute-start(bf16[4,1,16,128]{3,2,1,0:T(8,128)(2,1)S(1)} %get-tuple-element.28), channel_id=1, source_target_pairs={{0,1},{1,2},{2,3},{4,5},{5,6},{6,7},{8,9},{9,10},{10,11},{12,13},{... | collective-permute-start | bytes 49160 | tf_op jit(solution)/shard_map/ppermute | solution.py:16
  68.7 1.2 %collective-permute-done.15 = bf16[4,1,16,128]{3,2,1,0:T(8,128)(2,1)S(1)} collective-permute-done((bf16[4,1,16,128]{3,2,1,0:T(8,128)(2,1)S(1)}, bf16[4,1,16,128]{3,2,1,0:T(8,128)(2,1)S(1)}, u32[]{:S(2)}, u32[]{:S(2)}) %collective-permute-start.15) | collective-permute-done | bytes 16416 | tf_op jit(solution)/shard_map/ppermute | solution.py:16
  71.6 1.3 %multiply_reduce_fusion = (f32[6,16]{1,0:T(8,128)S(1)}, f32[6,2,8,16,128]{4,3,2,1,0:T(8,128)}) fusion(f32[2,8,16,128]{3,2,1,0:T(8,128)S(1)} %multiply_subtract_fusion, f32[6]{0:T(128)S(1)} %get-tuple-element.5, f32[2,8,16,128]{3,2,1,0:T(8,128)S(1)} %get-tuple-element.12, f32[6]{0:T(128)S(1)} %get-tuple-element.6, f32[2,8,16,128]{3,2,1,0:T(8,128)S(1)} %get-tuple-element.16, ...), kind=kLoop, calls=%fused_computation | loop fusion | flops 2162592 | bytes 1442296 | tf_op jit(solution)/shard_map/reduce_sum | solution.py:88
  72.9 44.3 %psum.7 = f32[6,16]{1,0:T(8,128)S(1)} all-reduce(f32[6,16]{1,0:T(8,128)S(1)} %get-tuple-element.7), channel_id=1, replica_groups=mesh['gx'=8,'gy'=4] {'gx','gy'}, use_global_device_ids=true, to_apply=%region_1.2 | all-reduce | flops 96 | bytes 768 | tf_op jit(solution)/shard_map/psum | solution.py:89
  (84 shorter events, 15.0 us)
Async XLA Ops:
  0.6 18.8 %copy-start = (bf16[2,8,4,128,128]{4,3,2,1,0:T(8,128)(2,1)S(1)}, bf16[2,8,4,128,128]{4,3,2,1,0:T(8,128)(2,1)}, u32[]{:S(2)}) copy-start(bf16[2,8,4,128,128]{4,3,2,1,0:T(8,128)(2,1)} %param.9) | copy-start | bytes 6291460
  3.3 6.5 %collective-permute-start = (bf16[1,8,17,128]{3,2,1,0:T(8,128)(2,1)S(1)}, bf16[1,8,17,128]{3,2,1,0:T(8,128)(2,1)S(1)}, u32[]{:S(2)}, u32[]{:S(2)}) collective-permute-start(bf16[1,8,17,128]{3,2,1,0:T(8,128)(2,1)S(1)} %get-tuple-element.37), channel_id=1, source_target_pairs={{0,4},{4,8},{8,12},{12,16},{16,20},{20,24},{24,28},{1,5},{5,9},{9,... | collective-permute-start | bytes 104456 | tf_op jit(solution)/shard_map/ppermute | solution.py:16
  5.7 5.2 %collective-permute-start.1 = (bf16[1,8,17,128]{3,2,1,0:T(8,128)(2,1)S(1)}, bf16[1,8,17,128]{3,2,1,0:T(8,128)(2,1)S(1)}, u32[]{:S(2)}, u32[]{:S(2)}) collective-permute-start(bf16[1,8,17,128]{3,2,1,0:T(8,128)(2,1)S(1)} %get-tuple-element.38), channel_id=1, source_target_pairs={{4,0},{8,4},{12,8},{16,12},{20,16},{24,20},{28,24},{5,1},{9,5},{13... | collective-permute-start | bytes 104456 | tf_op jit(solution)/shard_map/ppermute | solution.py:17
  10.9 6.6 %collective-permute-start.2 = (bf16[4,1,17,128]{3,2,1,0:T(8,128)(2,1)S(1)}, bf16[4,1,17,128]{3,2,1,0:T(8,128)(2,1)S(1)}, u32[]{:S(2)}, u32[]{:S(2)}) collective-permute-start(bf16[4,1,17,128]{3,2,1,0:T(8,128)(2,1)S(1)} %get-tuple-element.23), channel_id=1, source_target_pairs={{1,0},{2,1},{3,2},{5,4},{6,5},{7,6},{9,8},{10,9},{11,10},{13,12},{... | collective-permute-start | bytes 52232 | tf_op jit(solution)/shard_map/ppermute | solution.py:17
  12.2 6.1 %collective-permute-start.3 = (bf16[4,1,17,128]{3,2,1,0:T(8,128)(2,1)S(1)}, bf16[4,1,17,128]{3,2,1,0:T(8,128)(2,1)S(1)}, u32[]{:S(2)}, u32[]{:S(2)}) collective-permute-start(bf16[4,1,17,128]{3,2,1,0:T(8,128)(2,1)S(1)} %get-tuple-element.24), channel_id=1, source_target_pairs={{0,1},{1,2},{2,3},{4,5},{5,6},{6,7},{8,9},{9,10},{10,11},{12,13},{... | collective-permute-start | bytes 52232 | tf_op jit(solution)/shard_map/ppermute | solution.py:16
  19.2 1.0 copy-start.1
  20.2 4.9 %collective-permute-start.4 = (bf16[1,8,16,128]{3,2,1,0:T(8,128)(2,1)S(1)}, bf16[1,8,16,128]{3,2,1,0:T(8,128)(2,1)S(1)}, u32[]{:S(2)}, u32[]{:S(2)}) collective-permute-start(bf16[1,8,16,128]{3,2,1,0:T(8,128)(2,1)S(1)} %get-tuple-element.43), channel_id=1, source_target_pairs={{0,4},{4,8},{8,12},{12,16},{16,20},{20,24},{24,28},{1,5},{5,9},{9,... | collective-permute-start | bytes 98312 | tf_op jit(solution)/shard_map/ppermute | solution.py:16
  23.8 4.8 %collective-permute-start.5 = (bf16[1,8,16,128]{3,2,1,0:T(8,128)(2,1)S(1)}, bf16[1,8,16,128]{3,2,1,0:T(8,128)(2,1)S(1)}, u32[]{:S(2)}, u32[]{:S(2)}) collective-permute-start(bf16[1,8,16,128]{3,2,1,0:T(8,128)(2,1)S(1)} %get-tuple-element.44), channel_id=1, source_target_pairs={{4,0},{8,4},{12,8},{16,12},{20,16},{24,20},{28,24},{5,1},{9,5},{13... | collective-permute-start | bytes 98312 | tf_op jit(solution)/shard_map/ppermute | solution.py:17
  28.6 6.2 %collective-permute-start.6 = (bf16[4,1,16,128]{3,2,1,0:T(8,128)(2,1)S(1)}, bf16[4,1,16,128]{3,2,1,0:T(8,128)(2,1)S(1)}, u32[]{:S(2)}, u32[]{:S(2)}) collective-permute-start(bf16[4,1,16,128]{3,2,1,0:T(8,128)(2,1)S(1)} %get-tuple-element.35), channel_id=1, source_target_pairs={{1,0},{2,1},{3,2},{5,4},{6,5},{7,6},{9,8},{10,9},{11,10},{13,12},{... | collective-permute-start | bytes 49160 | tf_op jit(solution)/shard_map/ppermute | solution.py:17
  29.9 6.3 %collective-permute-start.7 = (bf16[4,1,16,128]{3,2,1,0:T(8,128)(2,1)S(1)}, bf16[4,1,16,128]{3,2,1,0:T(8,128)(2,1)S(1)}, u32[]{:S(2)}, u32[]{:S(2)}) collective-permute-start(bf16[4,1,16,128]{3,2,1,0:T(8,128)(2,1)S(1)} %get-tuple-element.36), channel_id=1, source_target_pairs={{0,1},{1,2},{2,3},{4,5},{5,6},{6,7},{8,9},{9,10},{10,11},{12,13},{... | collective-permute-start | bytes 49160 | tf_op jit(solution)/shard_map/ppermute | solution.py:16
  38.0 5.0 %collective-permute-start.8 = (bf16[1,8,16,128]{3,2,1,0:T(8,128)(2,1)S(1)}, bf16[1,8,16,128]{3,2,1,0:T(8,128)(2,1)S(1)}, u32[]{:S(2)}, u32[]{:S(2)}) collective-permute-start(bf16[1,8,16,128]{3,2,1,0:T(8,128)(2,1)S(1)} %get-tuple-element.41), channel_id=1, source_target_pairs={{0,4},{4,8},{8,12},{12,16},{16,20},{20,24},{24,28},{1,5},{5,9},{9,... | collective-permute-start | bytes 98312 | tf_op jit(solution)/shard_map/ppermute | solution.py:16
  41.7 3.5 %collective-permute-start.9 = (bf16[1,8,16,128]{3,2,1,0:T(8,128)(2,1)S(1)}, bf16[1,8,16,128]{3,2,1,0:T(8,128)(2,1)S(1)}, u32[]{:S(2)}, u32[]{:S(2)}) collective-permute-start(bf16[1,8,16,128]{3,2,1,0:T(8,128)(2,1)S(1)} %get-tuple-element.42), channel_id=1, source_target_pairs={{4,0},{8,4},{12,8},{16,12},{20,16},{24,20},{28,24},{5,1},{9,5},{13... | collective-permute-start | bytes 98312 | tf_op jit(solution)/shard_map/ppermute | solution.py:17
  45.2 6.1 %collective-permute-start.10 = (bf16[4,1,16,128]{3,2,1,0:T(8,128)(2,1)S(1)}, bf16[4,1,16,128]{3,2,1,0:T(8,128)(2,1)S(1)}, u32[]{:S(2)}, u32[]{:S(2)}) collective-permute-start(bf16[4,1,16,128]{3,2,1,0:T(8,128)(2,1)S(1)} %get-tuple-element.31), channel_id=1, source_target_pairs={{1,0},{2,1},{3,2},{5,4},{6,5},{7,6},{9,8},{10,9},{11,10},{13,12},{... | collective-permute-start | bytes 49160 | tf_op jit(solution)/shard_map/ppermute | solution.py:17
  46.4 6.3 %collective-permute-start.11 = (bf16[4,1,16,128]{3,2,1,0:T(8,128)(2,1)S(1)}, bf16[4,1,16,128]{3,2,1,0:T(8,128)(2,1)S(1)}, u32[]{:S(2)}, u32[]{:S(2)}) collective-permute-start(bf16[4,1,16,128]{3,2,1,0:T(8,128)(2,1)S(1)} %get-tuple-element.32), channel_id=1, source_target_pairs={{0,1},{1,2},{2,3},{4,5},{5,6},{6,7},{8,9},{9,10},{10,11},{12,13},{... | collective-permute-start | bytes 49160 | tf_op jit(solution)/shard_map/ppermute | solution.py:16
  53.5 15.0 %copy-start.2 = (f32[6,5]{1,0:T(8,128)S(1)}, f32[6,5]{1,0:T(8,128)}, u32[]{:S(2)}) copy-start(f32[6,5]{1,0:T(8,128)} %param.14) | copy-start | bytes 364
  54.5 5.4 %collective-permute-start.12 = (bf16[1,8,16,128]{3,2,1,0:T(8,128)(2,1)S(1)}, bf16[1,8,16,128]{3,2,1,0:T(8,128)(2,1)S(1)}, u32[]{:S(2)}, u32[]{:S(2)}) collective-permute-start(bf16[1,8,16,128]{3,2,1,0:T(8,128)(2,1)S(1)} %get-tuple-element.39), channel_id=1, source_target_pairs={{0,4},{4,8},{8,12},{12,16},{16,20},{20,24},{24,28},{1,5},{5,9},{9,... | collective-permute-start | bytes 98312 | tf_op jit(solution)/shard_map/ppermute | solution.py:16
  58.6 3.7 %collective-permute-start.13 = (bf16[1,8,16,128]{3,2,1,0:T(8,128)(2,1)S(1)}, bf16[1,8,16,128]{3,2,1,0:T(8,128)(2,1)S(1)}, u32[]{:S(2)}, u32[]{:S(2)}) collective-permute-start(bf16[1,8,16,128]{3,2,1,0:T(8,128)(2,1)S(1)} %get-tuple-element.40), channel_id=1, source_target_pairs={{4,0},{8,4},{12,8},{16,12},{20,16},{24,20},{28,24},{5,1},{9,5},{13... | collective-permute-start | bytes 98312 | tf_op jit(solution)/shard_map/ppermute | solution.py:17
  62.4 6.4 %collective-permute-start.14 = (bf16[4,1,16,128]{3,2,1,0:T(8,128)(2,1)S(1)}, bf16[4,1,16,128]{3,2,1,0:T(8,128)(2,1)S(1)}, u32[]{:S(2)}, u32[]{:S(2)}) collective-permute-start(bf16[4,1,16,128]{3,2,1,0:T(8,128)(2,1)S(1)} %get-tuple-element.27), channel_id=1, source_target_pairs={{1,0},{2,1},{3,2},{5,4},{6,5},{7,6},{9,8},{10,9},{11,10},{13,12},{... | collective-permute-start | bytes 49160 | tf_op jit(solution)/shard_map/ppermute | solution.py:17
  63.6 6.3 %collective-permute-start.15 = (bf16[4,1,16,128]{3,2,1,0:T(8,128)(2,1)S(1)}, bf16[4,1,16,128]{3,2,1,0:T(8,128)(2,1)S(1)}, u32[]{:S(2)}, u32[]{:S(2)}) collective-permute-start(bf16[4,1,16,128]{3,2,1,0:T(8,128)(2,1)S(1)} %get-tuple-element.28), channel_id=1, source_target_pairs={{0,1},{1,2},{2,3},{4,5},{5,6},{6,7},{8,9},{9,10},{10,11},{12,13},{... | collective-permute-start | bytes 49160 | tf_op jit(solution)/shard_map/ppermute | solution.py:16
where the time goes:
time: 119 us; the launch traced here: 118 us
  blocking collectives  44.3 us (37%)
  starting transfers between devices  43.2 us (36%)
  waiting for transfers between devices  14 us (12%)
  other arithmetic  11.6 us (10%)
  matrix products  2.6 us (2%)
  between operations  1.96 us (2%)
    psum x1, blocking collectives, shards(): energy = lax.psum(local_sums, ('gx', 'gy')) / nodes  44.3 us
    ppermute x8, starting transfers between devices, with_halo(): before = lax.ppermute(last, axis, up)  32.9 us
    ppermute x8, starting transfers between devices, with_halo(): after = lax.ppermute(first, axis, down)  10.3 us
    ppermute x8, waiting for transfers between devices, with_halo(): after = lax.ppermute(first, axis, down)  9.19 us
    ppermute x8, waiting for transfers between devices, with_halo(): before = lax.ppermute(last, axis, up)  4.79 us
    select_n x16, other arithmetic, adjacency(): picked = jnp.where(kept, picked, jnp.zeros_like(picked))  3.91 us
    dot_general x4, matrix products, adjacency(): lax.dot_general(flat_inputs, flat_tiles, (((1, 3), (1, 3)), ((0,), (0,)))...  2.6 us
  transfers between devices with their start and end apart: 16, of which 8 were waited for; matrix products, arithmetic and copies ran while one was open for 2% of the time, Pallas kernels for 0%

commit v1 on v0

v1 whole, which is shorter than its diff:
```python
import functools

import jax
import jax.numpy as jnp
from jax import lax
from jax.experimental import pallas as pl
from jax.experimental.pallas import tpu as pltpu
from jax.sharding import PartitionSpec as P

DEG = 4
EDGE = 32
MESH = pl.DeviceIdType.MESH
NT = (((1,), (1,)), ((), ()))


def kernel(
    nx, ny, sig, tiles_hbm, tdir, tmask, live_rows, bound_rows, coef, bound,
    totals, energy,
    tiles, w_own, w_edge, own0, own, acc, cheb, slope, en_all, pads,
    tile_sem, send_sem, recv_sem, en_send, en_recv,
):
    ex, ey, chan, size = sig.shape
    slots = tiles.shape[2]
    scales = coef.shape[0]
    groups = size // EDGE
    n = nx * ny
    gx, gy = lax.axis_index("gx"), lax.axis_index("gy")
    me = gx * ny + gy
    blocks = [(i, j) for i in range(ex) for j in range(ey)]

    for r in range(DEG):
        pad = pads[r]
        for row in (0, ex + 1, ex + 2):
            pad[row] = jnp.zeros(pad.shape[1:], pad.dtype)
        for row in range(1, ex + 1):
            for col in (0, ey + 1):
                pad[row, col] = jnp.zeros(pad.shape[2:], pad.dtype)

    barrier = pltpu.get_barrier_semaphore()

    @pl.loop(1, n)
    def _(k):
        peer = lax.rem(me + k, n)
        pl.semaphore_signal(
            barrier, inc=1, device_id=(peer // ny, lax.rem(peer, ny)), device_id_type=MESH
        )

    def tile_copy(i, j):
        return pltpu.make_async_copy(
            tiles_hbm.at[i, j], tiles.at[i, j], tile_sem.at[i * ey + j]
        )

    for i, j in blocks:
        tile_copy(i, j).start()

    lane = lax.broadcasted_iota(jnp.int32, (1, size), 1)
    factor = 2.0 / jnp.full((1, size), bound[0], jnp.float32)

    def live_of(i, j):
        return (lane < live_rows[i, j]).astype(jnp.float32)

    def edge_of(i, j):
        return (lane < bound_rows[i, j]).astype(jnp.float32)

    def spread(v, i, j):
        v = v * edge_of(i, j)
        step = EDGE
        while step < size:
            v = v + pltpu.roll(v, step, 1)
            step *= 2
        return v.astype(jnp.bfloat16)

    first_row = lax.broadcasted_iota(jnp.int32, (chan, size), 0) == 0
    for b, (i, j) in enumerate(blocks):
        live = live_of(i, j)
        v = sig[i, j] * live
        cheb[0, b] = v
        ind = jnp.where(first_row, jnp.broadcast_to(live, (chan, size)), 0.0)
        joined = jnp.concatenate([v, ind], axis=0)
        own0[b] = joined.astype(jnp.bfloat16)
        pads[0][i + 1, j + 1] = spread(joined, i, j)

    pl.semaphore_wait(barrier, n - 1)

    sides = []
    for dx in (-1, 0, 1):
        for dy in (-1, 0, 1):
            if dx or dy:
                sides.append((dx, dy))

    def cut(d, extent, far):
        if d == 0:
            return pl.ds(1, extent)
        if far:
            return pl.ds(extent + 1 if d < 0 else 0, 1)
        return pl.ds(1 if d < 0 else extent, 1)

    def inside(dx, dy):
        ok = None
        for d, g, m in ((dx, gx, nx), (dy, gy, ny)):
            if d:
                here = g > 0 if d < 0 else g < m - 1
                ok = here if ok is None else jnp.logical_and(ok, here)
        return ok

    def halo(r, k, dx, dy):
        pad = pads[r]
        return pltpu.make_async_remote_copy(
            src_ref=pad.at[cut(dx, ex, False), cut(dy, ey, False)],
            dst_ref=pad.at[cut(dx, ex, True), cut(dy, ey, True)],
            send_sem=send_sem.at[r, k],
            recv_sem=recv_sem.at[r, k],
            device_id=(gx + dx, gy + dy),
            device_id_type=MESH,
        )

    order = sorted(range(len(sides)), key=lambda k: -abs(sides[k][0]) - abs(sides[k][1]))

    def send(r):
        for k in order:
            dx, dy = sides[k]

            @pl.when(inside(dx, dy))
            def _():
                halo(r, k, dx, dy).start()

    def receive(r):
        for k in order:
            dx, dy = sides[k]

            @pl.when(inside(-dx, -dy))
            def _():
                halo(r, k, dx, dy).wait_recv()

    def add_totals(k):
        for s in range(scales):
            c = coef[s, k] * (0.5 if k == 0 else 1.0)
            for b, (i, j) in enumerate(blocks):
                term = c * cheb[k, b]
                totals[s, i, j] = term if k == 0 else totals[s, i, j] + term

    def weights(i, j):
        b = i * ey + j
        total = None
        packed = None
        for s in range(slots):
            tile = tiles[i, j, s].astype(jnp.float32)
            used = jnp.logical_and(tmask[i, s, j] == 1, tdir[i, s, j] == 4)
            term = tile * jnp.where(used, 1.0, 0.0)
            total = term if total is None else total + term
            rolled = pltpu.roll(tile, s * EDGE, 1) if s else tile
            packed = rolled if packed is None else jnp.where(lane >= s * EDGE, rolled, packed)
        high = total.astype(jnp.bfloat16)
        w_own[b, :, :size] = high
        w_own[b, :, size:] = (total - high.astype(jnp.float32)).astype(jnp.bfloat16)
        w_edge[b] = packed.astype(jnp.bfloat16)

    def gather(r, i, j):
        pad = pads[r]
        picked = None
        for s in range(slots):
            d = tdir[i, s, j]
            ok = jnp.logical_and(tmask[i, s, j] == 1, d != 4)
            row = (d * 11) >> 5
            col = d - 3 * row
            cell = pad[jnp.where(ok, row + i, ex + 2), jnp.where(ok, col + j, 0)]
            group = jnp.logical_and(lane >= s * EDGE, lane < (s + 1) * EDGE)
            term = cell * group.astype(jnp.bfloat16)
            picked = term if picked is None else picked + term
        return picked

    for r in range(DEG):
        send(r)
        add_totals(r)
        for b, (i, j) in enumerate(blocks):
            if r == 0:
                tile_copy(i, j).wait()
                weights(i, j)
            mine = own0[b] if r == 0 else own[r - 1, b]
            acc[b, : mine.shape[0]] = lax.dot_general(
                jnp.concatenate([mine, mine], axis=1), w_own[b], NT,
                preferred_element_type=jnp.float32,
            )
        receive(r)
        for b, (i, j) in enumerate(blocks):
            rows = 2 * chan if r == 0 else chan
            adj = acc[b, :rows] + lax.dot_general(
                gather(r, i, j), w_edge[b], NT, preferred_element_type=jnp.float32
            )
            scale = factor * live_of(i, j)
            v = cheb[r, b]
            if r == 0:
                slope[b] = scale * adj[chan : chan + 1] - 1.0
                following = slope[b] * v - scale * adj[:chan]
            else:
                following = 2.0 * (slope[b] * v - scale * adj) - cheb[r - 1, b]
            cheb[r + 1, b] = following
            if r < DEG - 1:
                own[r, b] = following.astype(jnp.bfloat16)
                pads[r + 1][i + 1, j + 1] = spread(following, i, j)

    sums = []
    for s in range(scales):
        c = coef[s, DEG]
        part = jnp.zeros((chan, size), jnp.float32)
        for b, (i, j) in enumerate(blocks):
            t = totals[s, i, j] + c * cheb[DEG, b]
            totals[s, i, j] = t
            part = part + t * t
        sums.append(part)

    width = en_all.shape[2]
    if width > scales * chan:
        sums.append(jnp.zeros((width - scales * chan, size), jnp.float32))
    local = lax.dot_general(
        jnp.ones((8, size), jnp.float32), jnp.concatenate(sums, axis=0), NT,
        precision=lax.Precision.HIGHEST, preferred_element_type=jnp.float32,
    )
    en_all[me] = local[:1]

    def share(k, slot):
        peer = lax.rem(me + k, n)
        return pltpu.make_async_remote_copy(
            src_ref=en_all.at[slot],
            dst_ref=en_all.at[slot],
            send_sem=en_send.at[k],
            recv_sem=en_recv.at[slot],
            device_id=(peer // ny, lax.rem(peer, ny)),
            device_id_type=MESH,
        )

    @pl.loop(1, n)
    def _(k):
        share(k, me).start()

    @pl.loop(1, n)
    def _(k):
        share(k, lax.rem(me + k, n)).wait_recv()

    total = jnp.sum(en_all[...], axis=0) * (1.0 / (ex * ey * size * n))
    for s in range(scales):
        energy[s : s + 1, :] = total[:, s * chan : (s + 1) * chan]

    @pl.loop(1, n)
    def _(k):
        share(k, me).wait_send()

    for r in range(DEG):
        for k in order:
            dx, dy = sides[k]

            @pl.when(inside(dx, dy))
            def _():
                halo(r, k, dx, dy).wait_send()


def solution(mesh):
    nx, ny = mesh.shape["gx"], mesh.shape["gy"]
    n = nx * ny

    def shards(
        signals, tiles, tile_dir, tile_mask, live_rows, bound_rows, scale_coeffs, spectral_bound
    ):
        ex, ey, chan, size = signals.shape
        slots = tiles.shape[2]
        scales = scale_coeffs.shape[0]
        nb = ex * ey
        width = -(-scales * chan // 128) * 128
        bf, f32 = jnp.bfloat16, jnp.float32
        vmem = pl.BlockSpec(memory_space=pltpu.VMEM)
        smem = pl.BlockSpec(memory_space=pltpu.SMEM)
        hbm = pl.BlockSpec(memory_space=pltpu.HBM)
        return pl.pallas_call(
            functools.partial(kernel, nx, ny),
            out_shape=(
                jax.ShapeDtypeStruct((scales, ex, ey, chan, size), f32),
                jax.ShapeDtypeStruct((scales, chan), f32),
            ),
            in_specs=[vmem, hbm] + [smem] * 6,
            out_specs=(vmem, vmem),
            scratch_shapes=[
                pltpu.VMEM((ex, ey, slots, size, size), bf),
                pltpu.VMEM((nb, size, 2 * size), bf),
                pltpu.VMEM((nb, size, size), bf),
                pltpu.VMEM((nb, 2 * chan, size), bf),
                pltpu.VMEM((DEG - 1, nb, chan, size), bf),
                pltpu.VMEM((nb, 2 * chan, size), f32),
                pltpu.VMEM((DEG + 1, nb, chan, size), f32),
                pltpu.VMEM((nb, 1, size), f32),
                pltpu.VMEM((n, 1, width), f32),
                [
                    pltpu.VMEM((ex + 3, ey + 2, chan * (2 if r == 0 else 1), size), bf)
                    for r in range(DEG)
                ],
                pltpu.SemaphoreType.DMA((nb,)),
                pltpu.SemaphoreType.DMA((DEG, 8)),
                pltpu.SemaphoreType.DMA((DEG, 8)),
                pltpu.SemaphoreType.DMA((n,)),
                pltpu.SemaphoreType.DMA((n,)),
            ],
            compiler_params=pltpu.CompilerParams(
                collective_id=0, has_side_effects=True, vmem_limit_bytes=40 * 1024 * 1024
            ),
        )(
            signals, tiles, jnp.swapaxes(tile_dir, 1, 2), jnp.swapaxes(tile_mask, 1, 2),
            live_rows, bound_rows, scale_coeffs, spectral_bound,
        )

    placed = (
        P("gx", "gy", None, None),
        P("gx", "gy", None, None, None),
        P("gx", "gy", None),
        P("gx", "gy", None),
        P("gx", "gy"),
        P("gx", "gy"),
        P(),
        P(),
    )
    return jax.shard_map(
        shards,
        mesh=mesh,
        in_specs=placed,
        out_specs=(P(None, "gx", "gy", None, None), P()),
        check_vma=False,
    )
```

time: 119 us -> 38 us (0.32)
  blocking collectives: 44.3 us -> 0 us
  starting transfers between devices: 43.2 us -> 0 us
  Pallas kernels: 0 us -> 29 us
  waiting for transfers between devices: 14 us -> 0 us
  other arithmetic: 11.6 us -> 0 us
  local copies, waits for them, and re-layouts: 0.2 us -> 7.38 us
  matrix products: 2.6 us -> 0 us
    psum x1 -> x0, blocking collectives: 44.3 us -> none  [shards(): energy = lax.psum(local_sums, ('gx', 'gy')) / nodes]
    ppermute x16 -> x0, starting transfers between devices: 43.2 us -> none  [the longest x8 32.9 us: with_halo(): before = lax.ppermute(last, axis, up)]
    pallas_call x0 -> x1, Pallas kernels: none -> 29 us  [shards(): pl.pallas_call(functools.partial(kernel, nx, ny), out_shape=(jax.ShapeDty...]
    ppermute x16 -> x0, waiting for transfers between devices: 14 us -> none  [the longest x8 9.19 us: with_halo(): after = lax.ppermute(first, axis, down)]
    unnamed x27 -> x16, local copies, waits for them, and re-layouts: 0.16 us -> 7.38 us
    select_n x16 -> x0, other arithmetic: 3.91 us -> none  [adjacency(): picked = jnp.where(kept, picked, jnp.zeros_like(picked))]
    dot_general x4 -> x0, matrix products: 2.6 us -> none  [adjacency(): lax.dot_general(flat_inputs, flat_tiles, (((1, 3), (1, 3)), ((0,), (0,)))...]
    eq x3 -> x0, other arithmetic: 2.5 us -> none  [the longest x2 1.66 us: adjacency(): matches = (tile_dir[:, :, slot_index] == direction)[:, :, None, None]]
  transfers between devices with their start and end apart: 16 -> 0, of which waited for: 8 -> 0; matrix products, arithmetic and copies ran while one was open for 2% -> 0% of each run, Pallas kernels for 0% -> 0%
where the time goes in v1:
time: 38 us; the launch traced here: 37.7 us
  Pallas kernels  29 us (76%)
  local copies, waits for them, and re-layouts  7.38 us (19%)
  between operations  1.3 us (3%)
    pallas_call x1, Pallas kernels, shards(): pl.pallas_call(functools.partial(kernel, nx, ny), out_shape=(jax.ShapeDty...  29 us
    unnamed x16, local copies, waits for them, and re-layouts  7.38 us

profile of v1, /device:TPU:0, one launch (start us, length us, event | category | flops | bytes accessed | tf_op | source)
XLA Modules:
  0.0 37.7 jit_solution(13166598996865218791)
XLA Ops:
  1.3 0.0 copy-start
  1.3 1.6 %copy-done = bf16[2,8,4,128,128]{4,3,2,1,0:T(8,128)(2,1)S(1)} copy-done((bf16[2,8,4,128,128]{4,3,2,1,0:T(8,128)(2,1)S(1)}, bf16[2,8,4,128,128]{4,3,2,1,0:T(8,128)(2,1)}, u32[]{:S(2)}) %copy-start) | copy-done | bytes 2097176
  2.9 0.0 copy-start.1
  2.9 0.9 %copy-done.1 = f32[2,8,16,128]{3,2,1,0:T(8,128)S(1)} copy-done((f32[2,8,16,128]{3,2,1,0:T(8,128)S(1)}, f32[2,8,16,128]{3,2,1,0:T(8,128)}, u32[]{:S(2)}) %copy-start.1) | copy-done | bytes 131096
  3.8 0.0 copy-start.2
  3.8 0.7 %copy-done.2 = s32[2,8,4]{1,2,0:T(4,128)S(1)} copy-done((s32[2,8,4]{1,2,0:T(4,128)S(1)}, s32[2,8,4]{1,2,0:T(4,128)}, u32[]{:S(2)}) %copy-start.2) | copy-done | bytes 280
  4.5 0.0 copy-start.3
  4.5 0.7 %copy-done.3 = s32[2,8,4]{1,2,0:T(4,128)S(1)} copy-done((s32[2,8,4]{1,2,0:T(4,128)S(1)}, s32[2,8,4]{1,2,0:T(4,128)}, u32[]{:S(2)}) %copy-start.3) | copy-done | bytes 280
  5.2 0.0 copy-start.4
  5.2 0.7 %copy-done.4 = f32[6,5]{1,0:T(8,128)S(1)} copy-done((f32[6,5]{1,0:T(8,128)S(1)}, f32[6,5]{1,0:T(8,128)}, u32[]{:S(2)}) %copy-start.4) | copy-done | bytes 144
  5.8 0.0 copy-start.5
  5.8 0.7 %copy-done.5 = s32[2,8]{1,0:T(2,128)S(1)} copy-done((s32[2,8]{1,0:T(2,128)S(1)}, s32[2,8]{1,0:T(2,128)}, u32[]{:S(2)}) %copy-start.5) | copy-done | bytes 88
  6.5 0.0 copy-start.6
  6.5 0.7 %copy-done.6 = s32[2,8]{1,0:T(2,128)S(1)} copy-done((s32[2,8]{1,0:T(2,128)S(1)}, s32[2,8]{1,0:T(2,128)}, u32[]{:S(2)}) %copy-start.6) | copy-done | bytes 88
  7.2 29.0 %shard_map.95 = (f32[6,2,8,16,128]{4,3,2,1,0:T(8,128)S(1)}, f32[6,16]{1,0:T(8,128)S(1)}) custom-call(f32[2,8,16,128]{3,2,1,0:T(8,128)S(1)} %copy-done.1, bf16[2,8,4,128,128]{4,3,2,1,0:T(8,128)(2,1)S(1)} %copy-done, s32[2,4,8]{2,1,0:T(4,128)S(1)} %bitcast.2, s32[2,4,8]{2,1,0:T(4,128)S(1)} %bitcast.3, s32[2,8]{1,0:T(2,128)S(1)} %copy-done.5, ...), custom_call_target="tpu_custom_call" | custom-call | tf_op jit(solution)/shard_map/pallas_call | solution.py:273
  36.2 0.9 %copy.13 = f32[6,2,8,16,128]{4,3,2,1,0:T(8,128)} copy(f32[6,2,8,16,128]{4,3,2,1,0:T(8,128)S(1)} %get-tuple-element.4) | data formatting | bytes 1572864
  37.1 0.6 %copy.14 = f32[6,16]{1,0:T(8,128)} copy(f32[6,16]{1,0:T(8,128)S(1)} %get-tuple-element.5) | data formatting | bytes 768
Async XLA Ops:
  1.3 1.6 %copy-start = (bf16[2,8,4,128,128]{4,3,2,1,0:T(8,128)(2,1)S(1)}, bf16[2,8,4,128,128]{4,3,2,1,0:T(8,128)(2,1)}, u32[]{:S(2)}) copy-start(bf16[2,8,4,128,128]{4,3,2,1,0:T(8,128)(2,1)} %tiles_hbm.1) | copy-start | bytes 6291460
  2.9 0.9 %copy-start.1 = (f32[2,8,16,128]{3,2,1,0:T(8,128)S(1)}, f32[2,8,16,128]{3,2,1,0:T(8,128)}, u32[]{:S(2)}) copy-start(f32[2,8,16,128]{3,2,1,0:T(8,128)} %sig.1) | copy-start | bytes 393220
  3.8 0.7 %copy-start.2 = (s32[2,8,4]{1,2,0:T(4,128)S(1)}, s32[2,8,4]{1,2,0:T(4,128)}, u32[]{:S(2)}) copy-start(s32[2,8,4]{1,2,0:T(4,128)} %param.10) | copy-start | bytes 772
  4.5 0.7 %copy-start.3 = (s32[2,8,4]{1,2,0:T(4,128)S(1)}, s32[2,8,4]{1,2,0:T(4,128)}, u32[]{:S(2)}) copy-start(s32[2,8,4]{1,2,0:T(4,128)} %param.11) | copy-start | bytes 772
  5.2 0.7 %copy-start.4 = (f32[6,5]{1,0:T(8,128)S(1)}, f32[6,5]{1,0:T(8,128)}, u32[]{:S(2)}) copy-start(f32[6,5]{1,0:T(8,128)} %coef.1) | copy-start | bytes 364
  5.8 0.7 %copy-start.5 = (s32[2,8]{1,0:T(2,128)S(1)}, s32[2,8]{1,0:T(2,128)}, u32[]{:S(2)}) copy-start(s32[2,8]{1,0:T(2,128)} %live_rows.1) | copy-start | bytes 196
  6.5 0.7 %copy-start.6 = (s32[2,8]{1,0:T(2,128)S(1)}, s32[2,8]{1,0:T(2,128)}, u32[]{:S(2)}) copy-start(s32[2,8]{1,0:T(2,128)} %bound_rows.1) | copy-start | bytes 196

commit v2 on v1

--- a/solution.py
+++ b/solution.py
@@ -8,16 +8,17 @@
 from jax.sharding import PartitionSpec as P
 
 DEG = 4
+VMEM_LIMIT = 67043328
 EDGE = 32
 MESH = pl.DeviceIdType.MESH
 NT = (((1,), (1,)), ((), ()))
 
 
 def kernel(
-    nx, ny, sig, tiles_hbm, tdir, tmask, live_rows, bound_rows, coef, bound,
+    nx, ny, sig_hbm, tiles_hbm, tdir_hbm, tmask_hbm, live_hbm, edge_hbm, coef_hbm, bound_hbm,
     totals, energy,
-    tiles, w_own, w_edge, own0, own, acc, cheb, slope, en_all, pads,
-    tile_sem, send_sem, recv_sem, en_send, en_recv,
+    sig, tdir, tmask, live_rows, bound_rows, coef, bound, tiles, w_own, w_edge, own0, own, acc, cheb, slope, en_all, pads,
+    tile_sem, send_sem, recv_sem, en_send, en_recv, in_sem,
 ):
     ex, ey, chan, size = sig.shape
     slots = tiles.shape[2]
@@ -38,12 +39,37 @@
 
     barrier = pltpu.get_barrier_semaphore()
 
-    @pl.loop(1, n)
-    def _(k):
-        peer = lax.rem(me + k, n)
-        pl.semaphore_signal(
-            barrier, inc=1, device_id=(peer // ny, lax.rem(peer, ny)), device_id_type=MESH
-        )
+    fetches = [
+        pltpu.make_async_copy(src, dst, in_sem.at[k])
+        for k, (src, dst) in enumerate(
+            [
+                (live_hbm, live_rows), (edge_hbm, bound_rows), (sig_hbm, sig), (tdir_hbm, tdir),
+                (tmask_hbm, tmask), (coef_hbm, coef), (bound_hbm, bound),
+            ]
+        )
+    ]
+    for copy in fetches:
+        copy.start()
+
+    def others(act):
+        def one(kx, px, ky):
+            py = gy + ky
+            act(kx * ny + ky, px, jnp.where(py >= ny, py - ny, py))
+
+        for ky in range(1, ny):
+            one(0, gx, ky)
+
+        @pl.loop(1, nx)
+        def _(kx):
+            px = gx + kx
+            px = jnp.where(px >= nx, px - nx, px)
+            for ky in range(ny):
+                one(kx, px, ky)
+
+    def greet(k, px, py):
+        pl.semaphore_signal(barrier, inc=1, device_id=(px, py), device_id_type=MESH)
+
+    others(greet)
 
     def tile_copy(i, j):
         return pltpu.make_async_copy(
@@ -53,8 +79,11 @@
     for i, j in blocks:
         tile_copy(i, j).start()
 
+    for copy in fetches:
+        copy.wait()
+
     lane = lax.broadcasted_iota(jnp.int32, (1, size), 1)
-    factor = 2.0 / jnp.full((1, size), bound[0], jnp.float32)
+    factor = 2.0 / jnp.full((1, size), bound[0, 0], jnp.float32)
 
     def live_of(i, j):
         return (lane < live_rows[i, j]).astype(jnp.float32)
@@ -115,10 +144,14 @@
         )
 
     order = sorted(range(len(sides)), key=lambda k: -abs(sides[k][0]) - abs(sides[k][1]))
-
-    def send(r):
+    corners = [(i, j) for i, j in blocks if i in (0, ex - 1) and j in (0, ey - 1)]
+    inner = [(i, j) for i, j in blocks if (i, j) not in corners]
+
+    def send(r, chosen):
         for k in order:
             dx, dy = sides[k]
+            if not chosen(dx, dy):
+                continue
 
             @pl.when(inside(dx, dy))
             def _():
@@ -169,8 +202,8 @@
             picked = term if picked is None else picked + term
         return picked
 
+    send(0, lambda dx, dy: True)
     for r in range(DEG):
-        send(r)
         add_totals(r)
         for b, (i, j) in enumerate(blocks):
             if r == 0:
@@ -182,7 +215,8 @@
                 preferred_element_type=jnp.float32,
             )
         receive(r)
-        for b, (i, j) in enumerate(blocks):
+        for i, j in corners + inner:
+            b = i * ey + j
             rows = 2 * chan if r == 0 else chan
             adj = acc[b, :rows] + lax.dot_general(
                 gather(r, i, j), w_edge[b], NT, preferred_element_type=jnp.float32
@@ -198,6 +232,10 @@
             if r < DEG - 1:
                 own[r, b] = following.astype(jnp.bfloat16)
                 pads[r + 1][i + 1, j + 1] = spread(following, i, j)
+                if (i, j) == corners[-1]:
+                    send(r + 1, lambda dx, dy: dx and dy)
+                if (i, j) == inner[-1]:
+                    send(r + 1, lambda dx, dy: not (dx and dy))
 
     sums = []
     for s in range(scales):
@@ -218,32 +256,24 @@
     )
     en_all[me] = local[:1]
 
-    def share(k, slot):
-        peer = lax.rem(me + k, n)
+    def share(k, slot, px, py):
         return pltpu.make_async_remote_copy(
             src_ref=en_all.at[slot],
             dst_ref=en_all.at[slot],
             send_sem=en_send.at[k],
             recv_sem=en_recv.at[slot],
-            device_id=(peer // ny, lax.rem(peer, ny)),
+            device_id=(px, py),
             device_id_type=MESH,
         )
 
-    @pl.loop(1, n)
-    def _(k):
-        share(k, me).start()
-
-    @pl.loop(1, n)
-    def _(k):
-        share(k, lax.rem(me + k, n)).wait_recv()
+    others(lambda k, px, py: share(k, me, px, py).start())
+    others(lambda k, px, py: share(k, px * ny + py, px, py).wait_recv())
 
     total = jnp.sum(en_all[...], axis=0) * (1.0 / (ex * ey * size * n))
     for s in range(scales):
         energy[s : s + 1, :] = total[:, s * chan : (s + 1) * chan]
 
-    @pl.loop(1, n)
-    def _(k):
-        share(k, me).wait_send()
+    others(lambda k, px, py: share(k, me, px, py).wait_send())
 
     for r in range(DEG):
         for k in order:
@@ -268,7 +298,6 @@
         width = -(-scales * chan // 128) * 128
         bf, f32 = jnp.bfloat16, jnp.float32
         vmem = pl.BlockSpec(memory_space=pltpu.VMEM)
-        smem = pl.BlockSpec(memory_space=pltpu.SMEM)
         hbm = pl.BlockSpec(memory_space=pltpu.HBM)
         return pl.pallas_call(
             functools.partial(kernel, nx, ny),
@@ -276,9 +305,16 @@
                 jax.ShapeDtypeStruct((scales, ex, ey, chan, size), f32),
                 jax.ShapeDtypeStruct((scales, chan), f32),
             ),
-            in_specs=[vmem, hbm] + [smem] * 6,
+            in_specs=[hbm] * 8,
             out_specs=(vmem, vmem),
             scratch_shapes=[
+                pltpu.VMEM(signals.shape, f32),
+                pltpu.SMEM((ex, slots, ey), jnp.int32),
+                pltpu.SMEM((ex, slots, ey), jnp.int32),
+                pltpu.SMEM((ex, ey), jnp.int32),
+                pltpu.SMEM((ex, ey), jnp.int32),
+                pltpu.SMEM(scale_coeffs.shape, f32),
+                pltpu.SMEM((1, 1), f32),
                 pltpu.VMEM((ex, ey, slots, size, size), bf),
                 pltpu.VMEM((nb, size, 2 * size), bf),
                 pltpu.VMEM((nb, size, size), bf),
@@ -297,13 +333,14 @@
                 pltpu.SemaphoreType.DMA((DEG, 8)),
                 pltpu.SemaphoreType.DMA((n,)),
                 pltpu.SemaphoreType.DMA((n,)),
+                pltpu.SemaphoreType.DMA((8,)),
             ],
             compiler_params=pltpu.CompilerParams(
-                collective_id=0, has_side_effects=True, vmem_limit_bytes=40 * 1024 * 1024
+                collective_id=0, has_side_effects=True, vmem_limit_bytes=VMEM_LIMIT
             ),
         )(
             signals, tiles, jnp.swapaxes(tile_dir, 1, 2), jnp.swapaxes(tile_mask, 1, 2),
-            live_rows, bound_rows, scale_coeffs, spectral_bound,
+            live_rows, bound_rows, scale_coeffs, spectral_bound.reshape(1, 1),
         )
 
     placed = (

time: 38 us -> 33.4 us (0.88)
  local copies, waits for them, and re-layouts: 7.38 us -> 3.33 us
  Pallas kernels: 29 us -> 28.6 us
    unnamed x16 -> x2, local copies, waits for them, and re-layouts: 7.38 us -> 3.33 us
    pallas_call x1, Pallas kernels: 29 us -> 28.6 us  [shards(): pl.pallas_call(functools.partial(kernel, nx, ny), out_shape=(jax.ShapeDty...]
where the time goes in v2:
time: 33.4 us; the launch traced here: 33.2 us
  Pallas kernels  28.6 us (86%)
  local copies, waits for them, and re-layouts  3.33 us (10%)
  between operations  1.29 us (4%)
    pallas_call x1, Pallas kernels, shards(): pl.pallas_call(functools.partial(kernel, nx, ny), out_shape=(jax.ShapeDty...  28.6 us
    unnamed x2, local copies, waits for them, and re-layouts  3.33 us

profile of v2, /device:TPU:0, one launch (start us, length us, event | category | flops | bytes accessed | tf_op | source)
XLA Modules:
  0.0 33.2 jit_solution(6800429980738673079)
XLA Ops:
  1.3 28.6 %shard_map.95 = (f32[6,2,8,16,128]{4,3,2,1,0:T(8,128)}, f32[6,16]{1,0:T(8,128)}) custom-call(f32[2,8,16,128]{3,2,1,0:T(8,128)} %sig_hbm.1, bf16[2,8,4,128,128]{4,3,2,1,0:T(8,128)(2,1)} %tiles_hbm.1, s32[2,4,8]{2,1,0:T(4,128)} %bitcast.4, s32[2,4,8]{2,1,0:T(4,128)} %bitcast.5, s32[2,8]{1,0:T(2,128)} %live_hbm.1, s32[2,8]{1,0:T(2,128)} %edge_hbm.1, ...), custom_call_target="tpu_custom_call" | custom-call | tf_op jit(solution)/shard_map/pallas_call | solution.py:302
  29.9 2.1 %copy.13 = f32[6,2,8,16,128]{4,3,2,1,0:T(8,128)} copy(f32[6,2,8,16,128]{4,3,2,1,0:T(8,128)} %get-tuple-element.4) | data formatting | bytes 1572864
  31.9 1.3 %copy.14 = f32[6,16]{1,0:T(8,128)} copy(f32[6,16]{1,0:T(8,128)} %get-tuple-element.5) | data formatting | bytes 768

commit v3 on v2

--- a/solution.py
+++ b/solution.py
@@ -16,9 +16,9 @@
 
 def kernel(
     nx, ny, sig_hbm, tiles_hbm, tdir_hbm, tmask_hbm, live_hbm, edge_hbm, coef_hbm, bound_hbm,
-    totals, energy,
-    sig, tdir, tmask, live_rows, bound_rows, coef, bound, tiles, w_own, w_edge, own0, own, acc, cheb, slope, en_all, pads,
-    tile_sem, send_sem, recv_sem, en_send, en_recv, in_sem,
+    totals_hbm, energy,
+    totals, sig, tdir, tmask, live_rows, bound_rows, coef, bound, tiles, w_own, w_edge, own0, own, acc, cheb, slope, en_all, pads,
+    tile_sem, send_sem, recv_sem, en_send, en_recv, in_sem, out_sem,
 ):
     ex, ey, chan, size = sig.shape
     slots = tiles.shape[2]
@@ -237,6 +237,9 @@
                 if (i, j) == inner[-1]:
                     send(r + 1, lambda dx, dy: not (dx and dy))
 
+    def out_copy(s):
+        return pltpu.make_async_copy(totals.at[s], totals_hbm.at[s], out_sem.at[s])
+
     sums = []
     for s in range(scales):
         c = coef[s, DEG]
@@ -246,6 +249,7 @@
             totals[s, i, j] = t
             part = part + t * t
         sums.append(part)
+        out_copy(s).start()
 
     width = en_all.shape[2]
     if width > scales * chan:
@@ -282,6 +286,26 @@
             @pl.when(inside(dx, dy))
             def _():
                 halo(r, k, dx, dy).wait_send()
+
+    for s in range(scales):
+        out_copy(s).wait()
+
+
+def hand_out(made_hbm, energy_in, out_hbm, energy_out, held, held_energy, load_sem, store_sem):
+    count = held.shape[0]
+    loads = [
+        pltpu.make_async_copy(made_hbm.at[s], held.at[s], load_sem.at[s]) for s in range(count)
+    ] + [pltpu.make_async_copy(energy_in, held_energy, load_sem.at[count])]
+    stores = [
+        pltpu.make_async_copy(held.at[s], out_hbm.at[s], store_sem.at[s]) for s in range(count)
+    ] + [pltpu.make_async_copy(held_energy, energy_out, store_sem.at[count])]
+    for load in loads:
+        load.start()
+    for load, store in zip(loads, stores):
+        load.wait()
+        store.start()
+    for store in stores:
+        store.wait()
 
 
 def solution(mesh):
@@ -299,15 +323,16 @@
         bf, f32 = jnp.bfloat16, jnp.float32
         vmem = pl.BlockSpec(memory_space=pltpu.VMEM)
         hbm = pl.BlockSpec(memory_space=pltpu.HBM)
-        return pl.pallas_call(
+        made, energy = pl.pallas_call(
             functools.partial(kernel, nx, ny),
             out_shape=(
                 jax.ShapeDtypeStruct((scales, ex, ey, chan, size), f32),
                 jax.ShapeDtypeStruct((scales, chan), f32),
             ),
             in_specs=[hbm] * 8,
-            out_specs=(vmem, vmem),
+            out_specs=(hbm, vmem),
             scratch_shapes=[
+                pltpu.VMEM((scales, ex, ey, chan, size), f32),
                 pltpu.VMEM(signals.shape, f32),
                 pltpu.SMEM((ex, slots, ey), jnp.int32),
                 pltpu.SMEM((ex, slots, ey), jnp.int32),
@@ -334,6 +359,7 @@
                 pltpu.SemaphoreType.DMA((n,)),
                 pltpu.SemaphoreType.DMA((n,)),
                 pltpu.SemaphoreType.DMA((8,)),
+                pltpu.SemaphoreType.DMA((scales,)),
             ],
             compiler_params=pltpu.CompilerParams(
                 collective_id=0, has_side_effects=True, vmem_limit_bytes=VMEM_LIMIT
@@ -342,6 +368,21 @@
             signals, tiles, jnp.swapaxes(tile_dir, 1, 2), jnp.swapaxes(tile_mask, 1, 2),
             live_rows, bound_rows, scale_coeffs, spectral_bound.reshape(1, 1),
         )
+        return pl.pallas_call(
+            hand_out,
+            out_shape=(
+                jax.ShapeDtypeStruct(made.shape, f32), jax.ShapeDtypeStruct(energy.shape, f32)
+            ),
+            in_specs=[hbm] * 2,
+            out_specs=(hbm, hbm),
+            scratch_shapes=[
+                pltpu.VMEM(made.shape, f32),
+                pltpu.VMEM(energy.shape, f32),
+                pltpu.SemaphoreType.DMA((scales + 1,)),
+                pltpu.SemaphoreType.DMA((scales + 1,)),
+            ],
+            compiler_params=pltpu.CompilerParams(vmem_limit_bytes=VMEM_LIMIT),
+        )(made, energy)
 
     placed = (
         P("gx", "gy", None, None),

time: 33.4 us -> 31.8 us (0.952)
  local copies, waits for them, and re-layouts: 3.33 us -> 0 us
  Pallas kernels: 28.6 us -> 30.3 us
    unnamed x2 -> x0, local copies, waits for them, and re-layouts: 3.33 us -> none
    pallas_call x0 -> x1, Pallas kernels: none -> 1.99 us  [shards(): pl.pallas_call(hand_out, out_shape=(jax.ShapeDtypeStruct(made.shape, f32)...]
where the time goes in v3:
time: 31.8 us; the launch traced here: 31.6 us
  Pallas kernels  30.3 us (95%)
  between operations  1.29 us (4%)
    pallas_call x1, Pallas kernels, shards(): pl.pallas_call(functools.partial(kernel, nx, ny), out_shape=(jax.ShapeDty...  28.4 us
    pallas_call x1, Pallas kernels, shards(): pl.pallas_call(hand_out, out_shape=(jax.ShapeDtypeStruct(made.shape, f32)...  1.99 us

profile of v3, /device:TPU:0, one launch (start us, length us, event | category | flops | bytes accessed | tf_op | source)
XLA Modules:
  0.0 31.6 jit_solution(15559653400584765620)
XLA Ops:
  1.3 28.4 %shard_map.95 = (f32[6,2,8,16,128]{4,3,2,1,0:T(8,128)}, f32[6,16]{1,0:T(8,128)}) custom-call(f32[2,8,16,128]{3,2,1,0:T(8,128)} %sig_hbm.1, bf16[2,8,4,128,128]{4,3,2,1,0:T(8,128)(2,1)} %tiles_hbm.1, s32[2,4,8]{2,1,0:T(4,128)} %bitcast.4, s32[2,4,8]{2,1,0:T(4,128)} %bitcast.5, s32[2,8]{1,0:T(2,128)} %live_hbm.1, s32[2,8]{1,0:T(2,128)} %edge_hbm.1, ...), custom_call_target="tpu_custom_call" | custom-call | tf_op jit(solution)/shard_map/pallas_call | solution.py:326
  29.6 2.0 %shard_map.96 = (f32[6,2,8,16,128]{4,3,2,1,0:T(8,128)}, f32[6,16]{1,0:T(8,128)}) custom-call(f32[6,2,8,16,128]{4,3,2,1,0:T(8,128)} %get-tuple-element.4.made_hbm, f32[6,16]{1,0:T(8,128)} %get-tuple-element.5.energy_in), custom_call_target="tpu_custom_call" | custom-call | tf_op jit(solution)/shard_map/pallas_call | solution.py:371

commit v4 on v3

--- a/solution.py
+++ b/solution.py
@@ -17,7 +17,7 @@
 def kernel(
     nx, ny, sig_hbm, tiles_hbm, tdir_hbm, tmask_hbm, live_hbm, edge_hbm, coef_hbm, bound_hbm,
     totals_hbm, energy,
-    totals, sig, tdir, tmask, live_rows, bound_rows, coef, bound, tiles, w_own, w_edge, own0, own, acc, cheb, slope, en_all, pads,
+    totals, sig, tdir, tmask, live_rows, bound_rows, coef, bound, tiles, w_own, w_edge, own0, own, acc, cheb, slope, en_all, pads, x_out, x_in,
     tile_sem, send_sem, recv_sem, en_send, en_recv, in_sem, out_sem,
 ):
     ex, ey, chan, size = sig.shape
@@ -36,6 +36,7 @@
         for row in range(1, ex + 1):
             for col in (0, ey + 1):
                 pad[row, col] = jnp.zeros(pad.shape[2:], pad.dtype)
+        x_in[r][...] = jnp.zeros(x_in[r].shape, x_in[r].dtype)
 
     barrier = pltpu.get_barrier_semaphore()
 
@@ -134,9 +135,15 @@
 
     def halo(r, k, dx, dy):
         pad = pads[r]
+        if dy == 0:
+            src = x_out[r].at[0 if dx < 0 else 1]
+            dst = x_in[r].at[1 if dx < 0 else 0]
+        else:
+            src = pad.at[cut(dx, ex, False), cut(dy, ey, False)]
+            dst = pad.at[cut(dx, ex, True), cut(dy, ey, True)]
         return pltpu.make_async_remote_copy(
-            src_ref=pad.at[cut(dx, ex, False), cut(dy, ey, False)],
-            dst_ref=pad.at[cut(dx, ex, True), cut(dy, ey, True)],
+            src_ref=src,
+            dst_ref=dst,
             send_sem=send_sem.at[r, k],
             recv_sem=recv_sem.at[r, k],
             device_id=(gx + dx, gy + dy),
@@ -164,6 +171,29 @@
             @pl.when(inside(-dx, -dy))
             def _():
                 halo(r, k, dx, dy).wait_recv()
+
+    def group_of(s):
+        return jnp.logical_and(lane >= s * EDGE, lane < (s + 1) * EDGE)
+
+    def pack(r, side):
+        row = 1 if side == 0 else ex
+        for q in range(x_out[r].shape[1]):
+            packed = None
+            for t in range(min(groups, ey - q * groups)):
+                term = pads[r][row, q * groups + t + 1] * group_of(t).astype(jnp.bfloat16)
+                packed = term if packed is None else packed + term
+            x_out[r][side, q] = packed
+
+    def unpack(r):
+        for side in (0, 1):
+            for j in range(ey):
+                v = x_in[r][side, j // groups].astype(jnp.float32)
+                v = jnp.where(group_of(j % groups), v, 0.0)
+                step = EDGE
+                while step < size:
+                    v = v + pltpu.roll(v, step, 1)
+                    step *= 2
+                pads[r][0 if side == 0 else ex + 1, j + 1] = v.astype(jnp.bfloat16)
 
     def add_totals(k):
         for s in range(scales):
@@ -197,12 +227,14 @@
             row = (d * 11) >> 5
             col = d - 3 * row
             cell = pad[jnp.where(ok, row + i, ex + 2), jnp.where(ok, col + j, 0)]
-            group = jnp.logical_and(lane >= s * EDGE, lane < (s + 1) * EDGE)
-            term = cell * group.astype(jnp.bfloat16)
+            term = cell * group_of(s).astype(jnp.bfloat16)
             picked = term if picked is None else picked + term
         return picked
 
-    send(0, lambda dx, dy: True)
+    send(0, lambda dx, dy: dy != 0)
+    pack(0, 0)
+    pack(0, 1)
+    send(0, lambda dx, dy: dy == 0)
     for r in range(DEG):
         add_totals(r)
         for b, (i, j) in enumerate(blocks):
@@ -215,6 +247,7 @@
                 preferred_element_type=jnp.float32,
             )
         receive(r)
+        unpack(r)
         for i, j in corners + inner:
             b = i * ey + j
             rows = 2 * chan if r == 0 else chan
@@ -233,9 +266,11 @@
                 own[r, b] = following.astype(jnp.bfloat16)
                 pads[r + 1][i + 1, j + 1] = spread(following, i, j)
                 if (i, j) == corners[-1]:
-                    send(r + 1, lambda dx, dy: dx and dy)
+                    send(r + 1, lambda dx, dy: dy and (dx or ex <= 2))
                 if (i, j) == inner[-1]:
-                    send(r + 1, lambda dx, dy: not (dx and dy))
+                    pack(r + 1, 0)
+                    pack(r + 1, 1)
+                    send(r + 1, lambda dx, dy: not (dy and (dx or ex <= 2)))
 
     def out_copy(s):
         return pltpu.make_async_copy(totals.at[s], totals_hbm.at[s], out_sem.at[s])
@@ -323,6 +358,12 @@
         bf, f32 = jnp.bfloat16, jnp.float32
         vmem = pl.BlockSpec(memory_space=pltpu.VMEM)
         hbm = pl.BlockSpec(memory_space=pltpu.HBM)
+        def packed():
+            quads = -(-ey * EDGE // size)
+            return [
+                pltpu.VMEM((2, quads, chan * (2 if r == 0 else 1), size), bf) for r in range(DEG)
+            ]
+
         made, energy = pl.pallas_call(
             functools.partial(kernel, nx, ny),
             out_shape=(
@@ -353,6 +394,8 @@
                     pltpu.VMEM((ex + 3, ey + 2, chan * (2 if r == 0 else 1), size), bf)
                     for r in range(DEG)
                 ],
+                packed(),
+                packed(),
                 pltpu.SemaphoreType.DMA((nb,)),
                 pltpu.SemaphoreType.DMA((DEG, 8)),
                 pltpu.SemaphoreType.DMA((DEG, 8)),

time: 31.8 us -> 31.4 us (0.987)
  Pallas kernels: 30.3 us -> 29.9 us
    pallas_call x1, Pallas kernels: 28.4 us -> 27.9 us  [shards(): pl.pallas_call(functools.partial(kernel, nx, ny), out_shape=(jax.ShapeDty...]
where the time goes in v4:
time: 31.4 us; the launch traced here: 31.2 us
  Pallas kernels  29.9 us (95%)
  between operations  1.29 us (4%)
    pallas_call x1, Pallas kernels, shards(): pl.pallas_call(functools.partial(kernel, nx, ny), out_shape=(jax.ShapeDty...  27.9 us
    pallas_call x1, Pallas kernels, shards(): pl.pallas_call(hand_out, out_shape=(jax.ShapeDtypeStruct(made.shape, f32)...  1.99 us

profile of v4, /device:TPU:0, one launch (start us, length us, event | category | flops | bytes accessed | tf_op | source)
XLA Modules:
  0.0 31.2 jit_solution(9473480308818971716)
XLA Ops:
  1.3 27.9 %shard_map.95 = (f32[6,2,8,16,128]{4,3,2,1,0:T(8,128)}, f32[6,16]{1,0:T(8,128)}) custom-call(f32[2,8,16,128]{3,2,1,0:T(8,128)} %sig_hbm.1, bf16[2,8,4,128,128]{4,3,2,1,0:T(8,128)(2,1)} %tiles_hbm.1, s32[2,4,8]{2,1,0:T(4,128)} %bitcast.4, s32[2,4,8]{2,1,0:T(4,128)} %bitcast.5, s32[2,8]{1,0:T(2,128)} %live_hbm.1, s32[2,8]{1,0:T(2,128)} %edge_hbm.1, ...), custom_call_target="tpu_custom_call" | custom-call | tf_op jit(solution)/shard_map/pallas_call | solution.py:367
  29.2 2.0 %shard_map.96 = (f32[6,2,8,16,128]{4,3,2,1,0:T(8,128)}, f32[6,16]{1,0:T(8,128)}) custom-call(f32[6,2,8,16,128]{4,3,2,1,0:T(8,128)} %get-tuple-element.4.made_hbm, f32[6,16]{1,0:T(8,128)} %get-tuple-element.5.energy_in), custom_call_target="tpu_custom_call" | custom-call | tf_op jit(solution)/shard_map/pallas_call | solution.py:414
